TPU v7x, 32 devices: a whole 2x2x4 slice. The times are simulated.
32 devices in a mesh: leaf: 8 (over y, x, core), front: 4 (over z).
Axes of the slice: x: 2, y: 2, z: 4, core: 2. Of those that a mesh axis runs over, the one named last changes fastest.
Arguments:
- leaf_pivot_block: bfloat16 [8, 2048, 256], P('leaf', 'front'), may hold values from -6 to 6
- leaf_rest_block: bfloat16 [8, 512, 256], P('leaf', 'front'), may hold values from -6 to 6
- node_pivot_block: bfloat16 [8, 2048, 256], P('leaf', 'front'), may hold values from -6 to 6
- node_rest_block: bfloat16 [8, 512, 256], P('leaf', 'front'), may hold values from -6 to 6
- leaf_vectors_pivot: bfloat16 [8, 2, 2048, 2048], P('leaf', None, 'front'), may hold values from -0.125 to 0.125
- leaf_vectors_rest: bfloat16 [8, 2, 512, 2048], P('leaf', None, 'front'), may hold values from -0.125 to 0.125
- node_vectors_pivot: bfloat16 [8, 2, 2048, 2048], P('leaf', None, 'front'), may hold values from -0.125 to 0.125
- node_vectors_rest: bfloat16 [8, 2, 512, 2048], P('leaf', None, 'front'), may hold values from -0.125 to 0.125
- stack_place: int32 [8, 1024], P('leaf'), may hold values from 0 to 2559, as said below
- parent_columns: int32 [8, 2, 512], P('leaf'), may hold values from 0 to 2047, as said below
- coupling: bfloat16 [8, 2, 2048, 512], P('leaf', None, 'front'), may hold values from -0.125 to 0.125
- pivot_inverse: bfloat16 [8, 2, 2048, 2048], P('leaf', None, 'front'), may hold values from -0.125 to 0.125
Outputs:
- solution: bfloat16 [8, 2, 2048, 256], P('leaf', None, 'front')
- remainder: bfloat16 [8, 512, 256], P('leaf', 'front')
Inputs may be any that keep to these rules, and one draw needn't show every extreme that they name: `stack_place`: each group's row holds 1024 distinct stack rows. `parent_columns`: each group's row for each slot holds 512 distinct pivot columns.
All inputs are finite; a program needn't handle non-finite values.
Results may differ from a plain program's by a relative error of at most 0.024.
Values may be sent and summed in bfloat16 or wider, within the bound.
A program may use at most 64 MiB of HBM per device.

v0:
```python
import jax
import jax.numpy as jnp
from jax import lax
from jax.sharding import PartitionSpec as P

K = 2048
C = 512
LEVELS = 2


def from_behind(block, axis, distance):
    devices = range(lax.axis_size(axis))
    route = [((i - distance) % len(devices), i) for i in devices]
    return lax.ppermute(block, axis, route)


def added(first, second):
    return (first.astype(jnp.float32) + second.astype(jnp.float32)).astype(jnp.bfloat16)


def per_device(
    leaf_pivot_block,
    leaf_rest_block,
    node_pivot_block,
    node_rest_block,
    leaf_vectors_pivot,
    leaf_vectors_rest,
    node_vectors_pivot,
    node_vectors_rest,
    stack_place,
    parent_columns,
    coupling,
    pivot_inverse,
):
    subtree = 2**LEVELS
    front_index = lax.axis_index("front")
    pivot_count = leaf_vectors_pivot.shape[2]
    rest_count = leaf_vectors_rest.shape[2]

    def reflect(block_pivot, block_rest, vectors_pivot, vectors_rest):
        partial_value = jnp.einsum(
            "ik,ir->kr", vectors_pivot[1], block_pivot, preferred_element_type=jnp.float32
        )
        partial_value = partial_value + jnp.einsum(
            "ik,ir->kr", vectors_rest[1], block_rest, preferred_element_type=jnp.float32
        )
        summed = lax.psum(partial_value.astype(jnp.bfloat16), "front")
        pivots = block_pivot - jnp.dot(vectors_pivot[0], summed, preferred_element_type=jnp.float32)
        rest = block_rest - jnp.dot(vectors_rest[0], summed, preferred_element_type=jnp.float32)
        return (pivots.astype(jnp.bfloat16), rest.astype(jnp.bfloat16))

    inverse_map = (
        jnp.full((K + C,), -1, jnp.int32).at[stack_place[0]].set(jnp.arange(2 * C, dtype=jnp.int32))
    )
    pivot_rows = front_index * pivot_count + jnp.arange(pivot_count, dtype=jnp.int32)
    rest_rows = K + front_index * rest_count + jnp.arange(rest_count, dtype=jnp.int32)
    pivot_source = inverse_map[pivot_rows]
    rest_source = inverse_map[rest_rows]

    def assemble(left_part, right_part):
        left_whole, right_whole = (
            lax.all_gather(left_part, "front", axis=0, tiled=True),
            lax.all_gather(right_part, "front", axis=0, tiled=True),
        )
        joined = jnp.concatenate([left_whole, right_whole], axis=0)

        def fill_rows(own_rows, source):
            picked_rows = jnp.take(joined, jnp.maximum(source, 0), axis=0)
            return jnp.where((source >= 0)[:, None], picked_rows, own_rows)

        return (
            fill_rows(node_pivot_block[0], pivot_source),
            fill_rows(node_rest_block[0], rest_source),
        )

    def run_node(left_part, right_part):
        stack_pivots, stack_rest = assemble(left_part, right_part)
        return reflect(stack_pivots, stack_rest, node_vectors_pivot[0], node_vectors_rest[0])

    leaf_pivots, leaf_remainder = reflect(
        leaf_pivot_block[0], leaf_rest_block[0], leaf_vectors_pivot[0], leaf_vectors_rest[0]
    )
    left_part = from_behind(leaf_remainder, "leaf", 1)
    node_pivots, node_remainder = run_node(left_part, leaf_remainder)
    height = 2
    offset = 2 ** (height - 2)
    left_part = from_behind(node_remainder, "leaf", offset)
    right_part = from_behind(node_remainder, "leaf", -offset)
    node_pivots, node_remainder = run_node(left_part, right_part)
    root_part = from_behind(node_remainder, "leaf", -(subtree // 2))
    node_pivots, node_remainder = run_node(root_part, jnp.zeros_like(root_part))
    pivots_own = (leaf_pivots, node_pivots)

    def settle(which_slot, parent, columns):
        right_side = pivots_own[which_slot].astype(jnp.float32)
        if parent is not None:
            chosen = jnp.take(parent, columns, axis=0)
            right_side = right_side - jnp.dot(
                coupling[0, which_slot], chosen, preferred_element_type=jnp.float32
            )
        gathered = lax.all_gather(right_side.astype(jnp.bfloat16), "front", axis=0, tiled=True)
        result = jnp.dot(pivot_inverse[0, which_slot], gathered, preferred_element_type=jnp.float32)
        return result.astype(jnp.bfloat16)

    def fetch_parent(parent_part):
        return lax.all_gather(parent_part, "front", axis=0, tiled=True)

    node_solution = settle(1, None, None)
    for height in range(LEVELS, 0, -1):
        if height == LEVELS:
            parent_part = from_behind(node_solution, "leaf", subtree // 2)
        else:
            offset = 2 ** (height - 1)
            lower_part = from_behind(node_solution, "leaf", offset)
            higher_part = from_behind(node_solution, "leaf", -offset)
            parent_part = added(higher_part, lower_part)
        node_solution = settle(1, fetch_parent(parent_part), parent_columns[0, 1])
    from_right = from_behind(node_solution, "leaf", -1)
    parent_part = added(from_right, node_solution)
    leaf_solution = settle(0, fetch_parent(parent_part), parent_columns[0, 0])
    solution = jnp.stack([leaf_solution, node_solution])[None]
    return (solution, node_remainder[None])


def solution(mesh):
    in_specs = (
        P("leaf", "front", None),
        P("leaf", "front", None),
        P("leaf", "front", None),
        P("leaf", "front", None),
        P("leaf", None, "front", None),
        P("leaf", None, "front", None),
        P("leaf", None, "front", None),
        P("leaf", None, "front", None),
        P("leaf", None),
        P("leaf", None, None),
        P("leaf", None, "front", None),
        P("leaf", None, "front", None),
    )
    out_specs = (P("leaf", None, "front", None), P("leaf", "front", None))
    return jax.shard_map(
        per_device, mesh=mesh, in_specs=in_specs, out_specs=out_specs, check_vma=False
    )
```

profile of v0, /device:TPU:0, one launch (start us, length us, event | category | flops | bytes accessed | tf_op | source)
XLA Modules:
  0.0 573.9 jit_solution(2272695669670710660)
XLA Ops:
  8.8 3.4 fusion
  12.5 4.3 scatter_custom_fusion
  18.0 3.1 gather_fusion
  21.5 45.5 %all-reduce.6.cloned.1.call-done = bf16[2048,256]{1,0:T(8,128)(2,1)} async-done(((bf16[2048,256]{1,0:T(8,128)(2,1)}), bf16[2048,256]{1,0:T(8,128)(2,1)}) %all-reduce.6.cloned.1.call-update) | async-done | bytes 1048592 | tf_op jit(solution)/shard_map/psum | solution.py:47
  67.0 1.7 fusion.85
  68.8 13.3 %all_gather.38 = bf16[512,256]{0,1:T(8,128)(2,1)S(1)} all-gather(bf16[128,256]{0,1:T(8,128)(2,1)S(1)} %fusion.85), channel_id=1, replica_groups=mesh['leaf'=8,'front'=4] {'front'}, dimensions={0}, use_global_device_ids=true | all-gather | bytes 327680 | tf_op jit(solution)/shard_map/all_gather | solution.py:63
  82.1 13.2 %all_gather.37 = bf16[512,256]{0,1:T(8,128)(2,1)S(1)} all-gather(bf16[128,256]{0,1:T(8,128)(2,1)S(1)} %collective-permute-done), channel_id=1, replica_groups=mesh['leaf'=8,'front'=4] {'front'}, dimensions={0}, use_global_device_ids=true | all-gather | bytes 327680 | tf_op jit(solution)/shard_map/all_gather | solution.py:62
  96.4 2.0 gather_fusion.3
  99.1 3.3 fusion.6
  102.5 50.2 %all-reduce.8.cloned.1.call-done = bf16[2048,256]{0,1:T(8,128)(2,1)} async-done(((bf16[2048,256]{0,1:T(8,128)(2,1)}), bf16[2048,256]{0,1:T(8,128)(2,1)}) %all-reduce.8.cloned.1.call-update) | async-done | bytes 1048592 | tf_op jit(solution)/shard_map/psum | solution.py:47
  152.7 1.7 fusion.86
  154.4 2.6 collective-permute-start.2
  157.1 1.9 collective-permute-done.1
  159.0 12.8 %all_gather.39 = bf16[512,256]{0,1:T(8,128)(2,1)S(1)} all-gather(bf16[128,256]{0,1:T(8,128)(2,1)S(1)} %collective-permute-done.1), channel_id=1, replica_groups=mesh['leaf'=8,'front'=4] {'front'}, dimensions={0}, use_global_device_ids=true | all-gather | bytes 327680 | tf_op jit(solution)/shard_map/all_gather | solution.py:62
  171.8 12.8 %all_gather.40 = bf16[512,256]{0,1:T(8,128)(2,1)S(1)} all-gather(bf16[128,256]{0,1:T(8,128)(2,1)S(1)} %collective-permute-done.2), channel_id=1, replica_groups=mesh['leaf'=8,'front'=4] {'front'}, dimensions={0}, use_global_device_ids=true | all-gather | bytes 327680 | tf_op jit(solution)/shard_map/all_gather | solution.py:63
  185.7 2.0 gather_fusion.5
  188.3 3.3 fusion.5
  191.7 49.5 %all-reduce.10.cloned.1.call-done = bf16[2048,256]{0,1:T(8,128)(2,1)} async-done(((bf16[2048,256]{0,1:T(8,128)(2,1)}), bf16[2048,256]{0,1:T(8,128)(2,1)}) %all-reduce.10.cloned.1.call-update) | async-done | bytes 1048592 | tf_op jit(solution)/shard_map/psum | solution.py:47
  241.3 1.7 fusion.87
  242.9 2.4 collective-permute-start.3
  245.4 1.9 collective-permute-done.3
  247.3 13.4 %all_gather.41 = bf16[512,256]{0,1:T(8,128)(2,1)S(1)} all-gather(bf16[128,256]{0,1:T(8,128)(2,1)S(1)} %collective-permute-done.3), channel_id=1, replica_groups=mesh['leaf'=8,'front'=4] {'front'}, dimensions={0}, use_global_device_ids=true | all-gather | bytes 327680 | tf_op jit(solution)/shard_map/all_gather | solution.py:62
  261.7 2.0 gather_fusion.6
  264.3 3.3 fusion.4
  267.7 51.1 %all-reduce.12.cloned.1.call-done = bf16[2048,256]{0,1:T(8,128)(2,1)} async-done(((bf16[2048,256]{0,1:T(8,128)(2,1)}), bf16[2048,256]{0,1:T(8,128)(2,1)}) %all-reduce.12.cloned.1.call-update) | async-done | bytes 1048592 | tf_op jit(solution)/shard_map/psum | solution.py:47
  318.8 3.4 fusion.48
  322.3 27.3 %all-gather.8.cloned.1.call-done = bf16[2048,256]{0,1:T(8,128)(2,1)} async-done(((bf16[512,256]{0,1:T(8,128)(2,1)}), bf16[2048,256]{0,1:T(8,128)(2,1)}) %all-gather.8.cloned.1.call-update) | async-done | bytes 1048592 | tf_op jit(solution)/shard_map/all_gather | solution.py:101
  349.6 2.7 fusion.78
  353.8 7.0 %collective-permute-done.4 = bf16[512,256]{1,0:T(8,128)(2,1)S(1)} collective-permute-done((bf16[512,256]{1,0:T(8,128)(2,1)S(1)}, bf16[512,256]{1,0:T(8,128)(2,1)S(1)}, u32[]{:S(2)}, u32[]{:S(2)}) %collective-permute-start.4) | collective-permute-done | bytes 262176 | tf_op jit(solution)/shard_map/ppermute | solution.py:14
  361.7 27.0 %all-gather.10.cloned.1.call-done = bf16[2048,256]{1,0:T(8,128)(2,1)} async-done(((bf16[512,256]{1,0:T(8,128)(2,1)}), bf16[2048,256]{1,0:T(8,128)(2,1)}) %all-gather.10.cloned.1.call-update) | async-done | bytes 1048592 | tf_op jit(solution)/shard_map/all_gather | solution.py:106
  388.7 2.9 gather_fusion.8
  392.9 27.5 %all-gather.12.cloned.1.call-done = bf16[2048,256]{0,1:T(8,128)(2,1)} async-done(((bf16[512,256]{0,1:T(8,128)(2,1)}), bf16[2048,256]{0,1:T(8,128)(2,1)}) %all-gather.12.cloned.1.call-update) | async-done | bytes 1048592 | tf_op jit(solution)/shard_map/all_gather | solution.py:101
  420.4 2.7 fusion.75
  423.1 2.6 collective-permute-start.5
  425.8 5.1 collective-permute-done.6
  431.7 27.8 %all-gather.14.cloned.1.call-done = bf16[2048,256]{0,1:T(8,128)(2,1)} async-done(((bf16[512,256]{0,1:T(8,128)(2,1)}), bf16[2048,256]{0,1:T(8,128)(2,1)}) %all-gather.14.cloned.1.call-update) | async-done | bytes 1048592 | tf_op jit(solution)/shard_map/all_gather | solution.py:106
  461.0 2.6 gather_fusion.9
  463.6 2.1 fusion.58
  465.8 27.4 %all-gather.16.cloned.1.call-done = bf16[2048,256]{0,1:T(8,128)(2,1)} async-done(((bf16[512,256]{0,1:T(8,128)(2,1)}), bf16[2048,256]{0,1:T(8,128)(2,1)}) %all-gather.16.cloned.1.call-update) | async-done | bytes 1048592 | tf_op jit(solution)/shard_map/all_gather | solution.py:101
  493.2 2.7 fusion.66
  497.3 3.9 collective-permute-done.7
  502.1 2.3 fusion.54
  504.4 26.1 %all-gather.18.cloned.1.call-done = bf16[2048,256]{0,1:T(8,128)(2,1)} async-done(((bf16[512,256]{0,1:T(8,128)(2,1)}), bf16[2048,256]{0,1:T(8,128)(2,1)}) %all-gather.18.cloned.1.call-update) | async-done | bytes 1048592 | tf_op jit(solution)/shard_map/all_gather | solution.py:106
  532.0 2.0 gather_fusion.10
  534.0 2.2 fusion.57
  536.2 1.7 fusion.89
  538.6 25.1 %all-gather.20.cloned.1.call-done = bf16[2048,256]{1,0:T(8,128)(2,1)} async-done(((bf16[512,256]{1,0:T(8,128)(2,1)}), bf16[2048,256]{1,0:T(8,128)(2,1)}) %all-gather.20.cloned.1.call-update) | async-done | bytes 1048592 | tf_op jit(solution)/shard_map/all_gather | solution.py:101
  563.7 2.7 fusion.72
  (108 shorter events, 20.4 us)
Async XLA Ops:
  7.2 1.6 copy-start.12
  7.2 59.8 %all-reduce.6.cloned.1.call-start = ((), (), s32[]{:S(2)}) async-start(), calls=%async_computation | async-start | bytes 2097152 | tf_op jit(solution)/shard_map/psum | solution.py:47
  8.8 3.5 copy-start.6
  8.8 3.7 copy-start.8
  12.2 8.9 %copy-start.7 = (bf16[1,128,256]{2,1,0:T(8,128)(2,1)S(1)}, bf16[1,128,256]{2,1,0:T(8,128)(2,1)}, u32[]{:S(2)}) copy-start(bf16[1,128,256]{2,1,0:T(8,128)(2,1)} %param.21) | copy-start | bytes 196612
  12.2 9.1 %copy-start.2 = (bf16[1,512,256]{2,1,0:T(8,128)(2,1)S(1)}, bf16[1,512,256]{2,1,0:T(8,128)(2,1)}, u32[]{:S(2)}) copy-start(bf16[1,512,256]{2,1,0:T(8,128)(2,1)} %param.20) | copy-start | bytes 786436
  12.2 54.8 %copy-start.5 = (bf16[1,2,128,2048]{3,2,1,0:T(8,128)(2,1)S(1)}, bf16[1,2,128,2048]{3,2,1,0:T(8,128)(2,1)}, u32[]{:S(2)}) copy-start(bf16[1,2,128,2048]{3,2,1,0:T(8,128)(2,1)} %param.23) | copy-start | bytes 3145732
  12.2 140.4 %all-reduce.8.cloned.1.call-start = ((), (), s32[]{:S(2)}) async-start(), calls=%async_computation.1 | async-start | bytes 2097152 | tf_op jit(solution)/shard_map/psum | solution.py:47
  68.7 13.4 %collective-permute-start = (bf16[128,256]{0,1:T(8,128)(2,1)S(1)}, bf16[128,256]{0,1:T(8,128)(2,1)S(1)}, u32[]{:S(2)}, u32[]{:S(2)}) collective-permute-start(bf16[128,256]{0,1:T(8,128)(2,1)S(1)} %fusion.85), channel_id=1, source_target_pairs={{28,0},{0,4},{4,8},{8,12},{12,16},{16,20},{20,24},{24,28},{29,1},{... | collective-permute-start | bytes 196616 | tf_op jit(solution)/shard_map/ppermute | solution.py:14
  95.4 3.3 copy-start
  102.5 138.8 %all-reduce.10.cloned.1.call-start = ((), (), s32[]{:S(2)}) async-start(), calls=%async_computation.2 | async-start | bytes 2097152 | tf_op jit(solution)/shard_map/psum | solution.py:47
  154.4 4.6 collective-permute-start.1
  154.4 17.4 %collective-permute-start.2 = (bf16[128,256]{0,1:T(8,128)(2,1)S(1)}, bf16[128,256]{0,1:T(8,128)(2,1)S(1)}, u32[]{:S(2)}, u32[]{:S(2)}) collective-permute-start(bf16[128,256]{0,1:T(8,128)(2,1)S(1)} %fusion.86), channel_id=1, source_target_pairs={{4,0},{8,4},{12,8},{16,12},{20,16},{24,20},{28,24},{0,28},{5,1},{9... | collective-permute-start | bytes 196616 | tf_op jit(solution)/shard_map/ppermute | solution.py:14
  191.7 127.1 %all-reduce.12.cloned.1.call-start = ((), (), s32[]{:S(2)}) async-start(), calls=%async_computation.3 | async-start | bytes 2097152 | tf_op jit(solution)/shard_map/psum | solution.py:47
  242.9 4.3 collective-permute-start.3
  267.7 81.9 %all-gather.8.cloned.1.call-start = ((), (), s32[]{:S(2)}) async-start(), calls=%async_computation.4 | async-start | bytes 1310720 | tf_op jit(solution)/shard_map/all_gather | solution.py:101
  322.2 39.4 %copy-start.9 = (s32[1,2,512]{2,1,0:T(2,128)S(1)}, s32[1,2,512]{2,1,0:T(2,128)}, u32[]{:S(2)}) copy-start(s32[1,2,512]{2,1,0:T(2,128)} %param.27) | copy-start | bytes 12292
  322.2 66.5 %all-gather.10.cloned.1.call-start = ((), (), s32[]{:S(2)}) async-start(), calls=%async_computation.5 | async-start | bytes 1310720 | tf_op jit(solution)/shard_map/all_gather | solution.py:106
  352.3 39.4 %copy-start.1 = (bf16[1,2,512,512]{3,2,1,0:T(8,128)(2,1)S(1)}, bf16[1,2,512,512]{3,2,1,0:T(8,128)(2,1)}, u32[]{:S(2)}) copy-start(bf16[1,2,512,512]{3,2,1,0:T(8,128)(2,1)} %param.28) | copy-start | bytes 3145732
  352.3 39.4 %copy-start.3 = (bf16[512,256]{0,1:T(8,128)(2,1)S(1)}, bf16[512,256]{0,1:T(8,128)(2,1)}, u32[]{:S(2)}) copy-start(bf16[512,256]{0,1:T(8,128)(2,1)} %fusion.48) | copy-start | bytes 786436
  352.3 8.5 %collective-permute-start.4 = (bf16[512,256]{1,0:T(8,128)(2,1)S(1)}, bf16[512,256]{1,0:T(8,128)(2,1)S(1)}, u32[]{:S(2)}, u32[]{:S(2)}) collective-permute-start(bf16[512,256]{1,0:T(8,128)(2,1)S(1)} %fusion.78), channel_id=1, source_target_pairs={{24,0},{28,4},{0,8},{4,12},{8,16},{12,20},{16,24},{20,28},{25,1},{... | collective-permute-start | bytes 786440 | tf_op jit(solution)/shard_map/ppermute | solution.py:14
  360.8 0.7 copy-start.4
  361.6 58.8 %all-gather.12.cloned.1.call-start = ((), (), s32[]{:S(2)}) async-start(), calls=%async_computation.6 | async-start | bytes 1310720 | tf_op jit(solution)/shard_map/all_gather | solution.py:101
  361.7 31.2 %copy-start.10 = (pred[512]{0:T(512)(128)(4,1)}, pred[512]{0:T(512)(128)(4,1)S(1)}, u32[]{:S(2)}) copy-start(pred[512]{0:T(512)(128)(4,1)S(1)} %compare_and_fusion.1) | copy-start | bytes 1540
  392.9 66.6 %all-gather.14.cloned.1.call-start = ((), (), s32[]{:S(2)}) async-start(), calls=%async_computation.7 | async-start | bytes 1310720 | tf_op jit(solution)/shard_map/all_gather | solution.py:106
  423.1 7.8 %collective-permute-start.6 = (bf16[512,256]{0,1:T(8,128)(2,1)S(1)}, bf16[512,256]{0,1:T(8,128)(2,1)S(1)}, u32[]{:S(2)}, u32[]{:S(2)}) collective-permute-start(bf16[512,256]{0,1:T(8,128)(2,1)S(1)} %fusion.75), channel_id=1, source_target_pairs={{28,0},{0,4},{4,8},{8,12},{12,16},{16,20},{20,24},{24,28},{29,1},{... | collective-permute-start | bytes 786440 | tf_op jit(solution)/shard_map/ppermute | solution.py:14
  423.1 7.7 %collective-permute-start.5 = (bf16[512,256]{0,1:T(8,128)(2,1)S(1)}, bf16[512,256]{0,1:T(8,128)(2,1)S(1)}, u32[]{:S(2)}, u32[]{:S(2)}) collective-permute-start(bf16[512,256]{0,1:T(8,128)(2,1)S(1)} %fusion.75), channel_id=1, source_target_pairs={{4,0},{8,4},{12,8},{16,12},{20,16},{24,20},{28,24},{0,28},{5,1},{9... | collective-permute-start | bytes 786440 | tf_op jit(solution)/shard_map/ppermute | solution.py:14
  431.6 61.6 %all-gather.16.cloned.1.call-start = ((), (), s32[]{:S(2)}) async-start(), calls=%async_computation.8 | async-start | bytes 1310720 | tf_op jit(solution)/shard_map/all_gather | solution.py:101
  465.7 36.4 %copy-start.11 = (bf16[2048,256]{1,0:T(8,128)(2,1)S(1)}, bf16[2048,256]{1,0:T(8,128)(2,1)}, u32[]{:S(2)}) copy-start(bf16[2048,256]{1,0:T(8,128)(2,1)} %all-reduce.6.cloned.1.call-done) | copy-start | bytes 3145732
  465.7 36.4 %copy-start.13 = (bf16[1,512,256]{2,1,0:T(8,128)(2,1)S(1)}, bf16[1,512,256]{2,1,0:T(8,128)(2,1)}, u32[]{:S(2)}) copy-start(bf16[1,512,256]{2,1,0:T(8,128)(2,1)} %param.18) | copy-start | bytes 786436
  465.8 64.8 %all-gather.18.cloned.1.call-start = ((), (), s32[]{:S(2)}) async-start(), calls=%async_computation.9 | async-start | bytes 1310720 | tf_op jit(solution)/shard_map/all_gather | solution.py:106
  495.9 5.3 collective-permute-start.7
  502.0 61.7 %all-gather.20.cloned.1.call-start = ((), (), s32[]{:S(2)}) async-start(), calls=%async_computation.10 | async-start | bytes 1310720 | tf_op jit(solution)/shard_map/all_gather | solution.py:101
Sparse Core Ops, SparseCore 0:
  12.4 54.6 all-reduce.5
  102.6 50.0 all-reduce.7
  191.8 49.4 all-reduce.9
  267.8 50.9 all-reduce.11
  322.3 27.2 all-gather.7
  361.7 27.0 all-gather.9
  393.0 27.3 all-gather.11
  431.7 27.6 all-gather.13
  465.9 27.3 all-gather.15
  502.1 28.3 all-gather.17
  536.3 27.3 all-gather.19
where the time goes:
time: 575 us; the launch traced here: 574 us
  waiting for transfers between devices  405 us (70%)
  blocking collectives  65.4 us (11%)
  matrix products  44.7 us (8%)
  local copies, waits for them, and re-layouts  31.7 us (6%)
  between operations  14.5 us (3%)
  starting transfers between devices  11.2 us (2%)
    psum x4, waiting for transfers between devices, reflect(): summed = lax.psum(partial_value.astype(jnp.bfloat16), 'front')  196 us
    all_gather x4, waiting for transfers between devices, settle(): lax.all_gather(right_side.astype(jnp.bfloat16), 'front', axis=0, tiled=True)  107 us
    all_gather x3, waiting for transfers between devices, fetch_parent(): return lax.all_gather(parent_part, 'front', axis=0, tiled=True)  81 us
    all_gather x3, blocking collectives, assemble(): lax.all_gather(left_part, 'front', axis=0, tiled=True)  39.3 us
    all_gather x2, blocking collectives, assemble(): lax.all_gather(right_part, 'front', axis=0, tiled=True)  26.1 us
    ppermute x8, waiting for transfers between devices, from_behind(): return lax.ppermute(block, axis, route)  19.8 us
    dot_general x4, matrix products, reflect(): jnp.einsum('ik,ir->kr', vectors_pivot[1], block_pivot, preferred_element_...  13.4 us
  transfers between devices with their start and end apart: 19, of which 16 were waited for; matrix products, arithmetic and copies ran while one was open for 2% of the time, Pallas kernels for 0%

commit v1 on v0

v1 whole, which is shorter than its diff:
```python
import jax
import jax.numpy as jnp
from jax import lax
from jax.sharding import PartitionSpec as P

LEVELS = 2


def from_behind(block, axis, distance):
    devices = range(lax.axis_size(axis))
    route = [((i - distance) % len(devices), i) for i in devices]
    return lax.ppermute(block, axis, route)


def added(first, second):
    return (first.astype(jnp.float32) + second.astype(jnp.float32)).astype(jnp.bfloat16)


def per_device(
    leaf_pivot_block,
    leaf_rest_block,
    node_pivot_block,
    node_rest_block,
    leaf_vectors_pivot,
    leaf_vectors_rest,
    node_vectors_pivot,
    node_vectors_rest,
    stack_place,
    parent_columns,
    coupling,
    pivot_inverse,
):
    subtree = 2**LEVELS
    front_index = lax.axis_index("front")
    pivot_count = leaf_vectors_pivot.shape[2]
    rest_count = leaf_vectors_rest.shape[2]
    depth = leaf_vectors_pivot.shape[3]
    rest_rows_all = stack_place.shape[1] // 2

    def dot32(first, second):
        return jnp.dot(first, second, preferred_element_type=jnp.float32)

    def reflect(block_pivot, block_rest, vectors_pivot, vectors_rest):
        partial_value = jnp.einsum(
            "ik,ir->kr", vectors_pivot[1], block_pivot, preferred_element_type=jnp.float32
        )
        partial_value = partial_value + jnp.einsum(
            "ik,ir->kr", vectors_rest[1], block_rest, preferred_element_type=jnp.float32
        )
        summed = lax.psum(partial_value.astype(jnp.bfloat16), "front")
        pivots = block_pivot - dot32(vectors_pivot[0], summed)
        rest = block_rest - dot32(vectors_rest[0], summed)
        return (pivots.astype(jnp.bfloat16), rest.astype(jnp.bfloat16))

    def one_hot(rows, places):
        return rows[:, None] == places[None, :]

    pivot_rows = front_index * pivot_count + jnp.arange(pivot_count, dtype=jnp.int32)
    rest_rows = depth + front_index * rest_count + jnp.arange(rest_count, dtype=jnp.int32)
    pivot_hits = one_hot(pivot_rows, stack_place[0])
    rest_hits = one_hot(rest_rows, stack_place[0])

    def assemble(joined):
        def fill_rows(own_rows, hits):
            count = joined.shape[0]
            picked_rows = dot32(hits[:, :count].astype(jnp.bfloat16), joined)
            filled = jnp.any(hits, axis=1)[:, None]
            return jnp.where(filled, picked_rows.astype(jnp.bfloat16), own_rows)

        return (fill_rows(node_pivot_block[0], pivot_hits), fill_rows(node_rest_block[0], rest_hits))

    rest_vectors = lax.all_gather(node_vectors_rest[0, 0], "front", axis=0, tiled=True)

    def product(vectors):
        value = jnp.einsum("ck,ik->ci", rest_vectors, vectors, preferred_element_type=jnp.float32)
        return value.astype(jnp.bfloat16)

    rest_by_pivot = product(node_vectors_pivot[0, 1])
    rest_by_rest = product(node_vectors_rest[0, 1])

    def pass_rest(left_whole, right_whole):
        stack_pivots, stack_rest = assemble(jnp.concatenate([left_whole, right_whole], axis=0))
        own = lax.dynamic_update_slice(
            jnp.zeros((rest_rows_all, stack_rest.shape[1]), jnp.float32),
            stack_rest.astype(jnp.float32),
            (front_index * rest_count, 0),
        )
        partial_value = own - dot32(rest_by_pivot, stack_pivots) - dot32(rest_by_rest, stack_rest)
        return lax.psum(partial_value.astype(jnp.bfloat16), "front")

    leaf_pivots, leaf_remainder = reflect(
        leaf_pivot_block[0], leaf_rest_block[0], leaf_vectors_pivot[0], leaf_vectors_rest[0]
    )
    whole = lax.all_gather(leaf_remainder, "front", axis=0, tiled=True)
    whole = pass_rest(from_behind(whole, "leaf", 1), whole)
    for height in range(2, LEVELS + 1):
        offset = 2 ** (height - 2)
        whole = pass_rest(from_behind(whole, "leaf", offset), from_behind(whole, "leaf", -offset))
    root_whole = from_behind(whole, "leaf", -(subtree // 2))
    stack_pivots, stack_rest = assemble(root_whole)
    node_pivots, node_remainder = reflect(
        stack_pivots, stack_rest, node_vectors_pivot[0], node_vectors_rest[0]
    )
    pivots_own = (leaf_pivots, node_pivots)

    def settle(which_slot, parent_part):
        right_side = pivots_own[which_slot].astype(jnp.float32)
        if parent_part is not None:
            hits = one_hot(parent_columns[0, which_slot], pivot_rows).astype(jnp.bfloat16)
            chosen = lax.psum(dot32(hits, parent_part).astype(jnp.bfloat16), "front")
            right_side = right_side - dot32(coupling[0, which_slot], chosen)
        gathered = lax.all_gather(right_side.astype(jnp.bfloat16), "front", axis=0, tiled=True)
        return dot32(pivot_inverse[0, which_slot], gathered).astype(jnp.bfloat16)

    node_solution = settle(1, None)
    for height in range(LEVELS, 0, -1):
        if height == LEVELS:
            parent_part = from_behind(node_solution, "leaf", subtree // 2)
        else:
            offset = 2 ** (height - 1)
            lower_part = from_behind(node_solution, "leaf", offset)
            higher_part = from_behind(node_solution, "leaf", -offset)
            parent_part = added(higher_part, lower_part)
        node_solution = settle(1, parent_part)
    from_right = from_behind(node_solution, "leaf", -1)
    parent_part = added(from_right, node_solution)
    leaf_solution = settle(0, parent_part)
    solution = jnp.stack([leaf_solution, node_solution])[None]
    return (solution, node_remainder[None])


def solution(mesh):
    in_specs = (
        P("leaf", "front", None),
        P("leaf", "front", None),
        P("leaf", "front", None),
        P("leaf", "front", None),
        P("leaf", None, "front", None),
        P("leaf", None, "front", None),
        P("leaf", None, "front", None),
        P("leaf", None, "front", None),
        P("leaf", None),
        P("leaf", None, None),
        P("leaf", None, "front", None),
        P("leaf", None, "front", None),
    )
    out_specs = (P("leaf", None, "front", None), P("leaf", "front", None))
    return jax.shard_map(
        per_device, mesh=mesh, in_specs=in_specs, out_specs=out_specs, check_vma=False
    )
```

time: 575 us -> 541 us (0.941)
  blocking collectives: 65.4 us -> 14.7 us
  waiting for transfers between devices: 405 us -> 446 us
  local copies, waits for them, and re-layouts: 31.7 us -> 3.58 us
  matrix products: 44.7 us -> 50.5 us
    psum x0 -> x5, waiting for transfers between devices: none -> 174 us  [the longest x3 104 us: settle(): chosen = lax.psum(dot32(hits, parent_part).astype(jnp.bfloat16), 'front')]
    psum x4 -> x2, waiting for transfers between devices: 196 us -> 106 us  [reflect(): summed = lax.psum(partial_value.astype(jnp.bfloat16), 'front')]
    all_gather x3 -> x1, waiting for transfers between devices: 81 us -> 24.6 us  [per_device(): lax.all_gather(node_vectors_rest[0, 0], 'front', axis=0, tiled=True)]
    all_gather x5 -> x1, blocking collectives: 65.4 us -> 14.7 us  [per_device(): whole = lax.all_gather(leaf_remainder, 'front', axis=0, tiled=True)]
    gather x17 -> x0, local copies, waits for them, and re-layouts: 20.9 us -> none  [the longest x12 9.17 us: fill_rows(): picked_rows = jnp.take(joined, jnp.maximum(source, 0), axis=0)]
    dot_general x13 -> x24, matrix products: 28.5 us -> 43.4 us  [the longest x22 36.7 us: dot32(): return jnp.dot(first, second, preferred_element_type=jnp.float32)]
    ppermute x8, waiting for transfers between devices: 19.8 us -> 31.6 us  [from_behind(): return lax.ppermute(block, axis, route)]
    dot_general x4 -> x2, matrix products: 13.4 us -> 5.16 us  [reflect(): jnp.einsum('ik,ir->kr', vectors_pivot[1], block_pivot, preferred_element_...]
  transfers between devices with their start and end apart: 19 -> 20, of which waited for: 16 -> 18; matrix products, arithmetic and copies ran while one was open for 2% -> 2% of each run, Pallas kernels for 0% -> 0%
where the time goes in v1:
time: 541 us
  waiting for transfers between devices  446 us (82%)
  matrix products  50.5 us (9%)
  blocking collectives  14.7 us (3%)
  between operations  14.5 us (3%)
  starting transfers between devices  11.1 us (2%)
    all_gather x4, waiting for transfers between devices, settle(): lax.all_gather(right_side.astype(jnp.bfloat16), 'front', axis=0, tiled=True)  109 us
    psum x2, waiting for transfers between devices, reflect(): summed = lax.psum(partial_value.astype(jnp.bfloat16), 'front')  106 us
    psum x3, waiting for transfers between devices, settle(): chosen = lax.psum(dot32(hits, parent_part).astype(jnp.bfloat16), 'front')  104 us
    psum x2, waiting for transfers between devices, pass_rest(): return lax.psum(partial_value.astype(jnp.bfloat16), 'front')  70.5 us
    dot_general x22, matrix products, dot32(): return jnp.dot(first, second, preferred_element_type=jnp.float32)  36.7 us
    ppermute x8, waiting for transfers between devices, from_behind(): return lax.ppermute(block, axis, route)  31.6 us
    all_gather x1, waiting for transfers between devices, per_device(): lax.all_gather(node_vectors_rest[0, 0], 'front', axis=0, tiled=True)  24.6 us
    all_gather x1, blocking collectives, per_device(): whole = lax.all_gather(leaf_remainder, 'front', axis=0, tiled=True)  14.7 us
  transfers between devices with their start and end apart: 20, of which 18 were waited for; matrix products, arithmetic and copies ran while one was open for 2% of the time, Pallas kernels for 0%

profile of v1, /device:TPU:0, one launch (start us, length us, event | category | flops | bytes accessed | tf_op | source)
XLA Modules:
  0.0 541.0 jit_solution(15112979476598378183)
XLA Ops:
  7.2 1.5 fusion.137
  8.8 3.5 fusion
  13.7 53.4 %all-reduce.8.cloned.1.call-done = bf16[2048,256]{1,0:T(8,128)(2,1)} async-done(((bf16[2048,256]{1,0:T(8,128)(2,1)}), bf16[2048,256]{1,0:T(8,128)(2,1)}) %all-reduce.8.cloned.1.call-update) | async-done | bytes 1048592 | tf_op jit(solution)/shard_map/psum | solution.py:50
  67.1 1.7 fusion.115
  68.8 14.7 %all_gather.18 = bf16[512,256]{0,1:T(8,128)(2,1)S(1)} all-gather(bf16[128,256]{0,1:T(8,128)(2,1)S(1)} %fusion.115), channel_id=1, replica_groups=mesh['leaf'=8,'front'=4] {'front'}, dimensions={0}, use_global_device_ids=true | all-gather | bytes 327680 | tf_op jit(solution)/shard_map/all_gather | solution.py:94
  84.0 6.2 %collective-permute-done = bf16[512,256]{0,1:T(8,128)(2,1)S(1)} collective-permute-done((bf16[512,256]{0,1:T(8,128)(2,1)S(1)}, bf16[512,256]{0,1:T(8,128)(2,1)S(1)}, u32[]{:S(2)}, u32[]{:S(2)}) %collective-permute-start) | collective-permute-done | bytes 262176 | tf_op jit(solution)/shard_map/ppermute | solution.py:12
  90.6 24.6 %all-gather.15.cloned.1.call-done = bf16[1,1,512,2048]{3,2,1,0:T(8,128)(2,1)} async-done(((bf16[1,1,128,2048]{3,2,1,0:T(8,128)(2,1)}), bf16[1,1,512,2048]{3,2,1,0:T(8,128)(2,1)}) %all-gather.15.cloned.1.call-update) | async-done | bytes 2097168 | tf_op jit(solution)/shard_map/all_gather | solution.py:72
  115.2 4.3 fusion.39
  119.5 2.1 convolution_subtract_fusion.3
  121.6 2.3 fusion.111
  123.9 0.9 fusion.65
  124.9 34.6 %all-reduce.10.cloned.1.call-done = bf16[512,256]{1,0:T(8,128)(2,1)} async-done(((bf16[512,256]{1,0:T(8,128)(2,1)}), bf16[512,256]{1,0:T(8,128)(2,1)}) %all-reduce.10.cloned.1.call-update) | async-done | bytes 262160 | tf_op jit(solution)/shard_map/psum | solution.py:89
  159.6 2.6 collective-permute-start.2
  162.2 5.3 collective-permute-done.1
  167.9 2.1 convolution_subtract_fusion.2
  170.9 35.9 %all-reduce.12.cloned.1.call-done = bf16[512,256]{1,0:T(8,128)(2,1)} async-done(((bf16[512,256]{1,0:T(8,128)(2,1)}), bf16[512,256]{1,0:T(8,128)(2,1)}) %all-reduce.12.cloned.1.call-update) | async-done | bytes 262160 | tf_op jit(solution)/shard_map/psum | solution.py:89
  206.8 2.4 collective-permute-start.3
  209.2 4.2 collective-permute-done.3
  214.4 1.4 copy-done
  215.8 1.7 fusion.2
  217.6 52.8 %all-reduce.14.cloned.1.call-done = bf16[2048,256]{0,1:T(8,128)(2,1)} async-done(((bf16[2048,256]{0,1:T(8,128)(2,1)}), bf16[2048,256]{0,1:T(8,128)(2,1)}) %all-reduce.14.cloned.1.call-update) | async-done | bytes 1048592 | tf_op jit(solution)/shard_map/psum | solution.py:50
  270.3 3.4 subtract_convert_fusion
  273.8 27.3 %all-gather.7.cloned.1.call-done = bf16[2048,256]{1,0:T(8,128)(2,1)} async-done(((bf16[512,256]{1,0:T(8,128)(2,1)}), bf16[2048,256]{1,0:T(8,128)(2,1)}) %all-gather.7.cloned.1.call-update) | async-done | bytes 1048592 | tf_op jit(solution)/shard_map/all_gather | solution.py:112
  301.1 2.7 fusion.108
  303.8 1.5 collective-permute-start.4
  305.3 7.0 %collective-permute-done.4 = bf16[512,256]{0,1:T(8,128)(2,1)S(1)} collective-permute-done((bf16[512,256]{0,1:T(8,128)(2,1)S(1)}, bf16[512,256]{0,1:T(8,128)(2,1)S(1)}, u32[]{:S(2)}, u32[]{:S(2)}) %collective-permute-start.4) | collective-permute-done | bytes 262176 | tf_op jit(solution)/shard_map/ppermute | solution.py:12
  312.3 1.1 fusion.67
  313.5 34.7 %all-reduce.16.cloned.1.call-done = bf16[512,256]{1,0:T(8,128)(2,1)} async-done(((bf16[512,256]{1,0:T(8,128)(2,1)}), bf16[512,256]{1,0:T(8,128)(2,1)}) %all-reduce.16.cloned.1.call-update) | async-done | bytes 262160 | tf_op jit(solution)/shard_map/psum | solution.py:110
  348.2 1.9 fusion.64
  350.2 28.0 %all-gather.9.cloned.1.call-done = bf16[2048,256]{1,0:T(8,128)(2,1)} async-done(((bf16[512,256]{1,0:T(8,128)(2,1)}), bf16[2048,256]{1,0:T(8,128)(2,1)}) %all-gather.9.cloned.1.call-update) | async-done | bytes 1048592 | tf_op jit(solution)/shard_map/all_gather | solution.py:112
  378.2 2.7 fusion.105
  381.0 2.6 collective-permute-start.5
  383.6 5.1 collective-permute-done.6
  388.7 1.1 fusion.70
  389.8 35.4 %all-reduce.18.cloned.1.call-done = bf16[512,256]{1,0:T(8,128)(2,1)} async-done(((bf16[512,256]{1,0:T(8,128)(2,1)}), bf16[512,256]{1,0:T(8,128)(2,1)}) %all-reduce.18.cloned.1.call-update) | async-done | bytes 262160 | tf_op jit(solution)/shard_map/psum | solution.py:110
  425.2 2.0 fusion.63
  427.3 27.9 %all-gather.11.cloned.1.call-done = bf16[2048,256]{1,0:T(8,128)(2,1)} async-done(((bf16[512,256]{1,0:T(8,128)(2,1)}), bf16[2048,256]{1,0:T(8,128)(2,1)}) %all-gather.11.cloned.1.call-update) | async-done | bytes 1048592 | tf_op jit(solution)/shard_map/all_gather | solution.py:112
  455.2 2.7 fusion.79
  457.9 1.4 collective-permute-start.7
  459.3 3.9 collective-permute-done.7
  463.2 1.1 convolution_convert_fusion
  464.3 2.6 fusion.59
  466.9 33.5 %all-reduce.20.cloned.1.call-done = bf16[512,256]{1,0:T(8,128)(2,1)} async-done(((bf16[512,256]{1,0:T(8,128)(2,1)}), bf16[512,256]{1,0:T(8,128)(2,1)}) %all-reduce.20.cloned.1.call-update) | async-done | bytes 262160 | tf_op jit(solution)/shard_map/psum | solution.py:110
  500.4 2.0 fusion.62
  502.4 2.3 fusion.164
  504.7 25.7 %all-gather.13.cloned.1.call-done = bf16[2048,256]{1,0:T(8,128)(2,1)} async-done(((bf16[512,256]{1,0:T(8,128)(2,1)}), bf16[2048,256]{1,0:T(8,128)(2,1)}) %all-gather.13.cloned.1.call-update) | async-done | bytes 1048592 | tf_op jit(solution)/shard_map/all_gather | solution.py:112
  530.4 2.7 fusion.102
  533.1 1.0 copy.21
  (72 shorter events, 5.2 us)
Async XLA Ops:
  7.2 1.6 copy-start.10
  7.2 59.9 %all-reduce.8.cloned.1.call-start = ((), (), s32[]{:S(2)}) async-start(), calls=%async_computation | async-start | bytes 2097152 | tf_op jit(solution)/shard_map/psum | solution.py:50
  8.8 3.6 copy-start.1
  12.2 1.0 copy-start.6
  12.3 1.2 copy-start.7
  12.3 54.8 %copy-start.4 = (bf16[1,2,128,2048]{3,2,1,0:T(8,128)(2,1)S(1)}, bf16[1,2,128,2048]{3,2,1,0:T(8,128)(2,1)}, u32[]{:S(2)}) copy-start(bf16[1,2,128,2048]{3,2,1,0:T(8,128)(2,1)} %param.17) | copy-start | bytes 3145732
  12.3 103.0 %all-gather.15.cloned.1.call-start = ((), (), s32[]{:S(2)}) async-start(), calls=%async_computation.11 | async-start | bytes 2621440 | tf_op jit(solution)/shard_map/all_gather | solution.py:72
  13.2 146.3 %all-reduce.10.cloned.1.call-start = ((), (), s32[]{:S(2)}) async-start(), calls=%async_computation.1 | async-start | bytes 524288 | tf_op jit(solution)/shard_map/psum | solution.py:89
  13.7 76.6 %copy-start.5 = (bf16[1,128,256]{2,1,0:T(8,128)(2,1)S(1)}, bf16[1,128,256]{2,1,0:T(8,128)(2,1)}, u32[]{:S(2)}) copy-start(bf16[1,128,256]{2,1,0:T(8,128)(2,1)} %param.15) | copy-start | bytes 196612
  83.5 6.7 %collective-permute-start = (bf16[512,256]{0,1:T(8,128)(2,1)S(1)}, bf16[512,256]{0,1:T(8,128)(2,1)S(1)}, u32[]{:S(2)}, u32[]{:S(2)}) collective-permute-start(bf16[512,256]{0,1:T(8,128)(2,1)S(1)} %all_gather.18), channel_id=1, source_target_pairs={{28,0},{0,4},{4,8},{8,12},{12,16},{16,20},{20,24},{24,28},{29,1},{... | collective-permute-start | bytes 786440 | tf_op jit(solution)/shard_map/ppermute | solution.py:12
  124.9 82.0 %all-reduce.12.cloned.1.call-start = ((), (), s32[]{:S(2)}) async-start(), calls=%async_computation.2 | async-start | bytes 524288 | tf_op jit(solution)/shard_map/psum | solution.py:89
  159.6 7.9 %collective-permute-start.1 = (bf16[512,256]{1,0:T(8,128)(2,1)}, bf16[512,256]{1,0:T(8,128)(2,1)S(1)}, u32[]{:S(2)}, u32[]{:S(2)}) collective-permute-start(bf16[512,256]{1,0:T(8,128)(2,1)} %all-reduce.10.cloned.1.call-done), channel_id=1, source_target_pairs={{28,0},{0,4},{4,8},{8,12},{12,16},{16,20},{20,24},{24,28},{29,1},{... | collective-permute-start | bytes 786440 | tf_op jit(solution)/shard_map/ppermute | solution.py:12
  159.6 8.0 %collective-permute-start.2 = (bf16[512,256]{1,0:T(8,128)(2,1)}, bf16[512,256]{1,0:T(8,128)(2,1)S(1)}, u32[]{:S(2)}, u32[]{:S(2)}) collective-permute-start(bf16[512,256]{1,0:T(8,128)(2,1)} %all-reduce.10.cloned.1.call-done), channel_id=1, source_target_pairs={{4,0},{8,4},{12,8},{16,12},{20,16},{24,20},{28,24},{0,28},{5,1},{9... | collective-permute-start | bytes 786440 | tf_op jit(solution)/shard_map/ppermute | solution.py:12
  169.9 44.1 %copy-start.9 = (bf16[1,512,256]{2,1,0:T(8,128)(2,1)S(1)}, bf16[1,512,256]{2,1,0:T(8,128)(2,1)}, u32[]{:S(2)}) copy-start(bf16[1,512,256]{2,1,0:T(8,128)(2,1)} %param.14) | copy-start | bytes 786436
  170.9 99.4 %all-reduce.14.cloned.1.call-start = ((), (), s32[]{:S(2)}) async-start(), calls=%async_computation.3 | async-start | bytes 2097152 | tf_op jit(solution)/shard_map/psum | solution.py:50
  206.8 6.6 %collective-permute-start.3 = (bf16[512,256]{1,0:T(8,128)(2,1)}, bf16[512,256]{1,0:T(8,128)(2,1)S(1)}, u32[]{:S(2)}, u32[]{:S(2)}) collective-permute-start(bf16[512,256]{1,0:T(8,128)(2,1)} %all-reduce.12.cloned.1.call-done), channel_id=1, source_target_pairs={{8,0},{12,4},{16,8},{20,12},{24,16},{28,20},{0,24},{4,28},{9,1},{1... | collective-permute-start | bytes 786440 | tf_op jit(solution)/shard_map/ppermute | solution.py:12
  213.6 2.2 copy-start
  217.5 83.6 %all-gather.7.cloned.1.call-start = ((), (), s32[]{:S(2)}) async-start(), calls=%async_computation.4 | async-start | bytes 1310720 | tf_op jit(solution)/shard_map/all_gather | solution.py:112
  273.7 31.6 %copy-start.8 = (s32[1,2,512]{2,1,0:T(2,128)S(1)}, s32[1,2,512]{2,1,0:T(2,128)}, u32[]{:S(2)}) copy-start(s32[1,2,512]{2,1,0:T(2,128)} %param.21) | copy-start | bytes 12292
  273.7 74.5 %copy-start.2 = (bf16[1,2,512,512]{3,2,1,0:T(8,128)(2,1)S(1)}, bf16[1,2,512,512]{3,2,1,0:T(8,128)(2,1)}, u32[]{:S(2)}) copy-start(bf16[1,2,512,512]{3,2,1,0:T(8,128)(2,1)} %param.22) | copy-start | bytes 3145732
  273.8 74.4 %copy-start.3 = (bf16[512,256]{1,0:T(8,128)(2,1)S(1)}, bf16[512,256]{1,0:T(8,128)(2,1)}, u32[]{:S(2)}) copy-start(bf16[512,256]{1,0:T(8,128)(2,1)} %subtract_convert_fusion) | copy-start | bytes 786436
  273.8 74.4 %all-reduce.16.cloned.1.call-start = ((), (), s32[]{:S(2)}) async-start(), calls=%async_computation.5 | async-start | bytes 524288 | tf_op jit(solution)/shard_map/psum | solution.py:110
  303.8 8.5 %collective-permute-start.4 = (bf16[512,256]{0,1:T(8,128)(2,1)S(1)}, bf16[512,256]{0,1:T(8,128)(2,1)S(1)}, u32[]{:S(2)}, u32[]{:S(2)}) collective-permute-start(bf16[512,256]{0,1:T(8,128)(2,1)S(1)} %fusion.108), channel_id=1, source_target_pairs={{24,0},{28,4},{0,8},{4,12},{8,16},{12,20},{16,24},{20,28},{25,1},{... | collective-permute-start | bytes 786440 | tf_op jit(solution)/shard_map/ppermute | solution.py:12
  313.4 64.8 %all-gather.9.cloned.1.call-start = ((), (), s32[]{:S(2)}) async-start(), calls=%async_computation.6 | async-start | bytes 1310720 | tf_op jit(solution)/shard_map/all_gather | solution.py:112
  350.2 75.1 %all-reduce.18.cloned.1.call-start = ((), (), s32[]{:S(2)}) async-start(), calls=%async_computation.7 | async-start | bytes 524288 | tf_op jit(solution)/shard_map/psum | solution.py:110
  380.9 7.8 %collective-permute-start.6 = (bf16[512,256]{0,1:T(8,128)(2,1)S(1)}, bf16[512,256]{0,1:T(8,128)(2,1)S(1)}, u32[]{:S(2)}, u32[]{:S(2)}) collective-permute-start(bf16[512,256]{0,1:T(8,128)(2,1)S(1)} %fusion.105), channel_id=1, source_target_pairs={{28,0},{0,4},{4,8},{8,12},{12,16},{16,20},{20,24},{24,28},{29,1},{... | collective-permute-start | bytes 786440 | tf_op jit(solution)/shard_map/ppermute | solution.py:12
  381.0 7.7 %collective-permute-start.5 = (bf16[512,256]{0,1:T(8,128)(2,1)S(1)}, bf16[512,256]{0,1:T(8,128)(2,1)S(1)}, u32[]{:S(2)}, u32[]{:S(2)}) collective-permute-start(bf16[512,256]{0,1:T(8,128)(2,1)S(1)} %fusion.105), channel_id=1, source_target_pairs={{4,0},{8,4},{12,8},{16,12},{20,16},{24,20},{28,24},{0,28},{5,1},{9... | collective-permute-start | bytes 786440 | tf_op jit(solution)/shard_map/ppermute | solution.py:12
  389.8 65.4 %all-gather.11.cloned.1.call-start = ((), (), s32[]{:S(2)}) async-start(), calls=%async_computation.8 | async-start | bytes 1310720 | tf_op jit(solution)/shard_map/all_gather | solution.py:112
  427.2 37.1 %copy-start.11 = (bf16[1,512,256]{2,1,0:T(8,128)(2,1)S(1)}, bf16[1,512,256]{2,1,0:T(8,128)(2,1)}, u32[]{:S(2)}) copy-start(bf16[1,512,256]{2,1,0:T(8,128)(2,1)} %param.12) | copy-start | bytes 786436
  427.2 73.2 %all-reduce.20.cloned.1.call-start = ((), (), s32[]{:S(2)}) async-start(), calls=%async_computation.9 | async-start | bytes 524288 | tf_op jit(solution)/shard_map/psum | solution.py:110
  457.9 5.3 collective-permute-start.7
  464.3 66.1 %all-gather.13.cloned.1.call-start = ((), (), s32[]{:S(2)}) async-start(), calls=%async_computation.10 | async-start | bytes 1310720 | tf_op jit(solution)/shard_map/all_gather | solution.py:112
Sparse Core Ops, SparseCore 0:
  12.4 54.6 all-reduce.7
  69.2 45.9 all-gather.14
  125.0 34.5 all-reduce.9
  171.0 35.7 all-reduce.11
  217.7 52.6 all-reduce.13
  273.9 27.2 all-gather.6
  313.5 34.6 all-reduce.15
  350.3 27.8 all-gather.8
  389.9 35.2 all-reduce.17
  427.3 27.8 all-gather.10
  464.4 35.9 all-reduce.19
  502.5 27.8 all-gather.12
